TPU v7x, 8 devices: a whole 2x2x1 slice. The times are simulated.
8 devices in a mesh: dp: 1 (over z), sp: 8 (over y, x, core).
Axes of the slice: x: 2, y: 2, z: 1, core: 2. Of those that a mesh axis runs over, the one named last changes fastest.
Arguments:
- x: bfloat16 [8192, 3072], P(('dp', 'sp'))
- grad_out: bfloat16 [8192, 3072], P(('dp', 'sp'))
- positions: int32 [8192], P(('dp', 'sp'))
- gain: bfloat16 [3072], replicated
- w_q: bfloat16 [3072, 3072], replicated
- w_k: bfloat16 [3072, 1024], replicated
- w_v: bfloat16 [3072, 1024], replicated
- w_o: bfloat16 [3072, 3072], replicated
Outputs:
- output 1: bfloat16 [8192, 3072], P(('dp', 'sp'))
- output 2: bfloat16 [8192, 3072], P(('dp', 'sp'))
- output 3: float32 [3072, 3072], P('dp')
- output 4: float32 [3072, 1024], P('dp')
- output 5: float32 [3072, 1024], P('dp')
- output 6: float32 [3072, 3072], P('dp')
- output 7: float32 [3072], P('dp')
All inputs are finite; a program needn't handle non-finite values.
Results may differ from a plain program's by a relative error of at most 0.02.
Values are sent between devices in bfloat16 or wider.
A program may use at most 1 GiB of HBM per device.

v0:
```python
import jax
import jax.numpy as jnp
from jax import lax
from jax.sharding import PartitionSpec as P

HEAD_DIM = 128
ROPE_THETA = 1000000.0
NORM_EPS = 1e-05
NEG_LARGE = -1e30
CONTRACT_ROWS = (((0,), (0,)), ((), ()))
CONTRACT_COLS = (((1,), (1,)), ((), ()))


def block_rows(seq_len, row_cost):
    row_count = seq_len
    while row_count > 8 and row_count * row_cost > 2 ** 24:
        row_count = row_count // 2
    return row_count


def rope_tables(positions):
    inv_freq = ROPE_THETA ** (-jnp.arange(0, HEAD_DIM, 2).astype(jnp.float32) / HEAD_DIM)
    angles = positions.astype(jnp.float32)[:, None] * inv_freq[None, :]
    return jnp.cos(angles)[:, None, :], jnp.sin(angles)[:, None, :]


def rotate(values, cos_t, sin_t):
    half_dim = values.shape[-1] // 2
    lower_half = values[..., :half_dim]
    upper_half = values[..., half_dim:]
    return jnp.concatenate([lower_half * cos_t - upper_half * sin_t, upper_half * cos_t + lower_half * sin_t], axis=-1)


def attn_forward(q_all, k_all, v_all):
    seq_len, kv_loc, group_size, head_dim = q_all.shape
    row_count = block_rows(seq_len, kv_loc * group_size * seq_len)
    n_blocks = seq_len // row_count
    qk_scale = head_dim ** -0.5
    key_index = jnp.arange(seq_len)
    q_blocks = q_all.reshape(n_blocks, row_count, kv_loc, group_size, head_dim)
    blk_starts = jnp.arange(n_blocks) * row_count

    def one_block(block_args):
        q_blk, blk_start = block_args
        scores = jnp.einsum('qhgd,khd->hgqk', q_blk, k_all, preferred_element_type=jnp.float32) * qk_scale
        causal = (blk_start + jnp.arange(row_count))[:, None] >= key_index[None, :]
        attn_prob = jax.nn.softmax(jnp.where(causal, scores, NEG_LARGE), axis=-1)
        blk_out = jnp.einsum('hgqk,khd->qhgd', attn_prob.astype(jnp.bfloat16), v_all, preferred_element_type=jnp.float32)
        return blk_out.astype(jnp.bfloat16)

    return lax.map(one_block, (q_blocks, blk_starts)).reshape(seq_len, kv_loc, group_size, head_dim)


def attn_backward(q_all, k_all, v_all, do_all):
    seq_len, kv_loc, group_size, head_dim = q_all.shape
    row_count = block_rows(seq_len, kv_loc * group_size * seq_len)
    n_blocks = seq_len // row_count
    qk_scale = head_dim ** -0.5
    key_index = jnp.arange(seq_len)
    q_blocks = q_all.reshape(n_blocks, row_count, kv_loc, group_size, head_dim)
    do_blocks = do_all.reshape(n_blocks, row_count, kv_loc, group_size, head_dim)
    blk_starts = jnp.arange(n_blocks) * row_count

    def one_block(acc_pair, block_args):
        dk_acc, dv_acc = acc_pair
        q_blk, do_blk, blk_start = block_args
        scores = jnp.einsum('qhgd,khd->hgqk', q_blk, k_all, preferred_element_type=jnp.float32) * qk_scale
        causal = (blk_start + jnp.arange(row_count))[:, None] >= key_index[None, :]
        attn_prob = jax.nn.softmax(jnp.where(causal, scores, NEG_LARGE), axis=-1)
        prob_bf = attn_prob.astype(jnp.bfloat16)
        dv_acc = dv_acc + jnp.einsum('hgqk,qhgd->khd', prob_bf, do_blk, preferred_element_type=jnp.float32)
        d_prob = jnp.einsum('qhgd,khd->hgqk', do_blk, v_all, preferred_element_type=jnp.float32)
        d_score = attn_prob * (d_prob - jnp.sum(attn_prob * d_prob, axis=-1, keepdims=True)) * qk_scale
        ds_bf = d_score.astype(jnp.bfloat16)
        dq_blk = jnp.einsum('hgqk,khd->qhgd', ds_bf, k_all, preferred_element_type=jnp.float32)
        dk_acc = dk_acc + jnp.einsum('hgqk,qhgd->khd', ds_bf, q_blk, preferred_element_type=jnp.float32)
        return (dk_acc, dv_acc), dq_blk.astype(jnp.bfloat16)

    zero_acc = jnp.zeros((seq_len, kv_loc, head_dim), jnp.float32)
    (dk_all, dv_all), dq_blocks = lax.scan(one_block, (zero_acc, zero_acc), (q_blocks, do_blocks, blk_starts))
    return dq_blocks.reshape(seq_len, kv_loc, group_size, head_dim), dk_all, dv_all


def solution(mesh):
    sp_size = mesh.shape['sp']
    seq_spec = P(('dp', 'sp'), None)
    pos_spec = P(('dp', 'sp'))
    replicated = P(None, None)
    part_rows = P('dp', None)

    def local_step(x, grad_out, positions, gain, w_q, w_k, w_v, w_o):
        tok_count = x.shape[0]
        n_heads = w_q.shape[1] // HEAD_DIM
        kv_heads = w_k.shape[1] // HEAD_DIM
        kv_copies = max(1, sp_size // kv_heads)
        q_loc = n_heads // sp_size
        kv_loc = max(kv_heads, sp_size) // sp_size
        group_size = q_loc // kv_loc
        seq_len = tok_count * sp_size
        x_f = x.astype(jnp.float32)
        inv_rms = lax.rsqrt(jnp.mean(x_f * x_f, axis=-1, keepdims=True) + NORM_EPS)
        normed = x_f * inv_rms
        gain_f = gain.astype(jnp.float32)
        hidden = (normed * gain_f).astype(jnp.bfloat16)
        cos_t, sin_t = rope_tables(positions)
        q_proj = jnp.dot(hidden, w_q, preferred_element_type=jnp.float32).reshape(tok_count, n_heads, HEAD_DIM)
        k_proj = jnp.dot(hidden, w_k, preferred_element_type=jnp.float32).reshape(tok_count, kv_heads, HEAD_DIM)
        v_send = jnp.dot(hidden, w_v, preferred_element_type=jnp.float32).astype(jnp.bfloat16).reshape(tok_count, kv_heads, HEAD_DIM)
        q_rot = rotate(q_proj, cos_t, sin_t).astype(jnp.bfloat16)
        k_send = rotate(k_proj, cos_t, sin_t).astype(jnp.bfloat16)
        if kv_copies > 1:
            k_send = jnp.repeat(k_send, kv_copies, axis=1)
            v_send = jnp.repeat(v_send, kv_copies, axis=1)
        q_all = lax.all_to_all(q_rot, 'sp', 1, 0, tiled=True).reshape(seq_len, kv_loc, group_size, HEAD_DIM)
        k_all = lax.all_to_all(k_send, 'sp', 1, 0, tiled=True)
        v_all = lax.all_to_all(v_send, 'sp', 1, 0, tiled=True)
        o_all = attn_forward(q_all, k_all, v_all)
        o_loc = lax.all_to_all(o_all.reshape(seq_len, q_loc, HEAD_DIM), 'sp', 0, 1, tiled=True).reshape(tok_count, n_heads * HEAD_DIM)
        mixed = jnp.dot(o_loc, w_o, preferred_element_type=jnp.float32)
        result = (x_f + mixed).astype(jnp.bfloat16)
        grad_wo = lax.psum(lax.dot_general(o_loc, grad_out, CONTRACT_ROWS, preferred_element_type=jnp.float32), 'sp')
        d_o = lax.dot_general(grad_out, w_o, CONTRACT_COLS, preferred_element_type=jnp.float32).astype(jnp.bfloat16)
        do_all = lax.all_to_all(d_o.reshape(tok_count, n_heads, HEAD_DIM), 'sp', 1, 0, tiled=True).reshape(seq_len, kv_loc, group_size, HEAD_DIM)
        dq_all, dk_all, dv_all = attn_backward(q_all, k_all, v_all, do_all)
        dq_loc = lax.all_to_all(dq_all.reshape(seq_len, q_loc, HEAD_DIM), 'sp', 0, 1, tiled=True)
        dk_loc = lax.all_to_all(dk_all.astype(jnp.bfloat16), 'sp', 0, 1, tiled=True)
        dv_loc = lax.all_to_all(dv_all.astype(jnp.bfloat16), 'sp', 0, 1, tiled=True)
        dk_sum = jnp.sum(dk_loc.reshape(tok_count, kv_heads, kv_copies, HEAD_DIM), axis=2, dtype=jnp.float32)
        dv_sum = jnp.sum(dv_loc.reshape(tok_count, kv_heads, kv_copies, HEAD_DIM), axis=2, dtype=jnp.float32)
        dq_pre = rotate(dq_loc.astype(jnp.float32), cos_t, -sin_t).astype(jnp.bfloat16).reshape(tok_count, n_heads * HEAD_DIM)
        dk_pre = rotate(dk_sum, cos_t, -sin_t).astype(jnp.bfloat16).reshape(tok_count, kv_heads * HEAD_DIM)
        dv_pre = dv_sum.astype(jnp.bfloat16).reshape(tok_count, kv_heads * HEAD_DIM)
        grad_wq = lax.psum(lax.dot_general(hidden, dq_pre, CONTRACT_ROWS, preferred_element_type=jnp.float32), 'sp')
        grad_wk = lax.psum(lax.dot_general(hidden, dk_pre, CONTRACT_ROWS, preferred_element_type=jnp.float32), 'sp')
        grad_wv = lax.psum(lax.dot_general(hidden, dv_pre, CONTRACT_ROWS, preferred_element_type=jnp.float32), 'sp')
        d_hidden = (lax.dot_general(dq_pre, w_q, CONTRACT_COLS, preferred_element_type=jnp.float32)
                    + lax.dot_general(dk_pre, w_k, CONTRACT_COLS, preferred_element_type=jnp.float32)
                    + lax.dot_general(dv_pre, w_v, CONTRACT_COLS, preferred_element_type=jnp.float32))
        grad_gain = lax.psum(jnp.sum(d_hidden * normed, axis=0), 'sp')
        d_normed = d_hidden * gain_f
        d_xnorm = inv_rms * (d_normed - normed * jnp.mean(d_normed * normed, axis=-1, keepdims=True))
        grad_x = (grad_out.astype(jnp.float32) + d_xnorm).astype(jnp.bfloat16)
        return result, grad_x, grad_wq, grad_wk, grad_wv, grad_wo, grad_gain

    return jax.shard_map(local_step, mesh=mesh,
                         in_specs=(seq_spec, seq_spec, pos_spec, P(None), replicated, replicated, replicated, replicated),
                         out_specs=(seq_spec, seq_spec, part_rows, part_rows, part_rows, part_rows, P('dp')),
                         check_vma=False)
```

profile of v0, /device:TPU:1, one launch (start us, length us, event | category | flops | bytes accessed | tf_op | source)
XLA Modules:
  0.0 5926.3 jit_solution(3036285169695288150)
XLA Ops:
  194.7 54.8 all-to-all-done
  260.0 2916.5 %while.27 = (s32[]{:T(128)}, f32[8192,1,128]{0,2,1:T(8,128)}, f32[8192,1,128]{0,2,1:T(8,128)}, bf16[16,512,1,3,128]{4,1,0,3,2:T(8,128)(2,1)}, bf16[16,512,1,3,12...) while((s32[]{:T(128)}, f32[8192,1,128]{0,2,1:T(8,128)}, ...), condition=%wide.region_9.10_spmd.clone, body=%wide.region_5.9_spmd.clone.sunk | while | flops 16441864192 | bytes 503257280 | solution.py:80
  372.3 41.3 fusion.159
  517.7 35.8 fusion.158
  553.5 41.3 fusion.159
  700.1 35.8 fusion.158
  735.9 41.3 fusion.159
  882.5 35.8 fusion.158
  918.3 41.3 fusion.159
  1100.6 41.3 fusion.159
  1283.0 41.3 fusion.159
  1465.4 41.3 fusion.159
  1647.7 41.3 fusion.159
  1830.1 41.3 fusion.159
  2012.5 41.3 fusion.159
  2194.9 41.3 fusion.159
  2377.2 41.3 fusion.159
  2559.6 41.3 fusion.159
  2742.0 41.3 fusion.159
  2924.4 41.3 fusion.159
  3106.7 41.3 fusion.159
  3228.7 1190.3 %while.26 = (s32[]{:T(128)}, bf16[16,512,1,3,128]{4,1,0,3,2:T(8,128)(2,1)}, s32[16]{0:T(128)}, bf16[16,512,1,3,128]{4,1,3,2,0:T(8,128)(2,1)}, bf16[8192,1,128]{2...) while((s32[]{:T(128)}, bf16[16,512,1,3,128]{4,1,0,3,2:T(8,128)(2,1)}, s32[16]{0:T(128)}, ...), condition=%wide.region_4.5_spmd.clone, body=%wide.region_1.4_spmd.clone.sunk | while | flops 6597834240 | bytes 197953712 | solution.py:51
  4443.7 79.8 %all-to-all-done.3 = bf16[8192,3,128]{2,1,0:T(4,128)(2,1)} async-done(((bf16[8192,3,128]{2,1,0:T(4,128)(2,1)}), bf16[8192,3,128]{2,1,0:T(4,128)(2,1)}, u32[]{:S(2)}, u32[]{:S(2)}) %all-to-all-start.3) | async-done | bytes 6291488 | tf_op jit(solution)/shard_map/all_to_all | solution.py:118
  4852.0 987.3 %all-reduce.3.cloned.1.call-done = (f32[3072,3072]{1,0:T(8,128)}, f32[3072,1024]{1,0:T(8,128)}, f32[3072,1024]{1,0:T(8,128)}, f32[3072,3072]{1,0:T(8,128)}) async-done(((f32[3072,3072]{1,0:T(8,128)}, f32[3072,1024]{1,0:T(8,128)}, f32[3072,1024]{1,0:T(8,128)}, f32[3072,3072]{1,0:T(8,128)}), (f32[3072,3072]{1,0:T(8,128)}, f32[3072,1024]{1,0:T(8,128)}, f32[3072,1024]{1,0:T(8,128)}, ...) | async-done | bytes 100663312 | tf_op jit(solution)/shard_map/psum | solution.py:133
  (508 shorter events, 4020.1 us)
Async XLA Ops:
  11.4 93.7 %copy-start.20 = (f32[1024]{0:T(1024)}, f32[1024]{0:T(1024)S(1)}, u32[]{:S(2)}) copy-start(f32[1024]{0:T(1024)S(1)} %add_rsqrt_fusion) | copy-start | bytes 12292
  11.8 93.4 %copy-start.18 = (f32[3072]{0:T(1024)}, f32[3072]{0:T(1024)S(1)}, u32[]{:S(2)}) copy-start(f32[3072]{0:T(1024)S(1)} %convert_element_type.123) | copy-start | bytes 36868
  22.1 26.7 all-to-all-start.2
  27.8 65.2 %copy-start.7 = (f32[1024,64]{0,1:T(8,128)}, f32[1024,64]{0,1:T(8,128)S(1)}, u32[]{:S(2)}) copy-start(f32[1024,64]{0,1:T(8,128)S(1)} %get-tuple-element.277) | copy-start | bytes 786436
  48.8 52.6 all-to-all-start.1
  93.2 65.6 %copy-start.5 = (f32[1024,64]{1,0:T(8,128)}, f32[1024,64]{1,0:T(8,128)S(1)}, u32[]{:S(2)}) copy-start(f32[1024,64]{1,0:T(8,128)S(1)} %copy.123) | copy-start | bytes 786436
  101.4 76.3 %all-to-all-start.4 = ((bf16[1024,24,128]{2,0,1:T(8,128)(2,1)}), bf16[1024,24,128]{2,0,1:T(8,128)(2,1)}, u32[]{:S(2)}, u32[]{:S(2)}) async-start(bf16[1024,24,128]{2,0,1:T(8,128)(2,1)} %bitcast.307), calls=%async_computation.4 | async-start | bytes 12582912 | tf_op jit(solution)/shard_map/all_to_all | solution.py:123
  177.7 71.7 %all-to-all-start = ((bf16[1024,24,128]{2,0,1:T(8,128)(2,1)}), bf16[1024,24,128]{2,0,1:T(8,128)(2,1)}, u32[]{:S(2)}, u32[]{:S(2)}) async-start(bf16[1024,24,128]{2,0,1:T(8,128)(2,1)} %pad_maximum_fusion), calls=%async_computation | async-start | bytes 12582912 | tf_op jit(solution)/shard_map/all_to_all | solution.py:114
  3188.8 28.8 all-to-all-start.6
  3217.6 1211.9 %all-to-all-start.7 = ((bf16[8,2,65536]{2,1,0:T(2,128)(2,1)}), bf16[8,2,65536]{2,1,0:T(2,128)(2,1)}, u32[]{:S(2)}, u32[]{:S(2)}) async-start(bf16[8,2,65536]{2,1,0:T(2,128)(2,1)} %reshape.260), calls=%async_computation.7 | async-start | bytes 4194304 | tf_op jit(solution)/shard_map/all_to_all | solution.py:127
  3234.0 23.4 copy-start.1
  3308.3 23.4 copy-start.1
  3457.0 23.4 copy-start.1
  3605.8 23.4 copy-start.1
  3754.5 23.4 copy-start.1
  4051.9 23.4 copy-start.1
  4429.5 94.0 %all-to-all-start.3 = ((bf16[8192,3,128]{2,1,0:T(4,128)(2,1)}), bf16[8192,3,128]{2,1,0:T(4,128)(2,1)}, u32[]{:S(2)}, u32[]{:S(2)}) async-start(bf16[8192,3,128]{2,1,0:T(4,128)(2,1)} %copy.131), calls=%async_computation.3 | async-start | bytes 16777216 | tf_op jit(solution)/shard_map/all_to_all | solution.py:118
  4443.7 87.2 %copy-start.9 = (f32[1024,64]{0,1:T(8,128)S(1)}, f32[1024,64]{0,1:T(8,128)}, u32[]{:S(2)}) copy-start(f32[1024,64]{0,1:T(8,128)} %get-tuple-element.275) | copy-start | bytes 786436
  4443.7 87.4 %copy-start.4 = (bf16[8,2,65536]{2,1,0:T(2,128)(2,1)S(1)}, bf16[8,2,65536]{2,1,0:T(2,128)(2,1)}, u32[]{:S(2)}) copy-start(bf16[8,2,65536]{2,1,0:T(2,128)(2,1)} %copy-done.3) | copy-start | bytes 6291460
  4523.5 97.7 %all-to-all-start.5 = ((bf16[8192,3,128]{2,1,0:T(4,128)(2,1)}), bf16[8192,3,128]{2,1,0:T(4,128)(2,1)}, u32[]{:S(2)}, u32[]{:S(2)}) async-start(bf16[8192,3,128]{2,1,0:T(4,128)(2,1)} %copy.139), calls=%async_computation.5 | async-start | bytes 16777216 | tf_op jit(solution)/shard_map/all_to_all | solution.py:125
  4530.9 1308.3 %all-reduce.3.cloned.1.call-start = ((), (), s32[]{:S(2)}) async-start(), calls=%async_computation.8 | async-start | bytes 201326592 | tf_op jit(solution)/shard_map/psum | solution.py:133
  4659.6 38.4 slice-start.4
  4668.4 29.7 slice-start.5
  4725.4 25.7 slice-start.2
  (75 other events, 1359.9 us)
Sparse Core Ops, SparseCore 0:
  4723.9 1115.3 all-reduce.2
where the time goes:
time: 5940 us; the launch traced here: 5930 us
  matrix products  2780 us (47%)
  other arithmetic  1610 us (27%)
  waiting for transfers between devices  1150 us (19%)
  local copies, waits for them, and re-layouts  286 us (5%)
    psum x1, waiting for transfers between devices, local_step(): lax.psum(lax.dot_general(hidden, dq_pre, CONTRACT_ROWS, preferred_element...  987 us
    dot_general x32, matrix products, one_block(): jnp.einsum('qhgd,khd->hgqk', q_blk, k_all, preferred_element_type=jnp.flo...  749 us
    reduce_sum x32, other arithmetic, one_block(): attn_prob = jax.nn.softmax(jnp.where(causal, scores, NEG_LARGE), axis=-1)  736 us
    another operation x20, other arithmetic  687 us
    dot_general x16, matrix products, one_block(): jnp.einsum('qhgd,khd->hgqk', do_blk, v_all, preferred_element_type=jnp.fl...  573 us
    dot_general x16, matrix products, one_block(): jnp.einsum('hgqk,qhgd->khd', prob_bf, do_blk, preferred_element_type=jnp....  412 us
    dot_general x16, matrix products, one_block(): jnp.einsum('hgqk,khd->qhgd', attn_prob.astype(jnp.bfloat16), v_all, prefe...  364 us
    dot_general x16, matrix products, one_block(): jnp.einsum('hgqk,qhgd->khd', ds_bf, q_blk, preferred_element_type=jnp.flo...  250 us
  transfers between devices with their start and end apart: 9, of which 6 were waited for; matrix products, arithmetic and copies ran while one was open for 26% of the time, Pallas kernels for 0%

commit v1 on v0

v1 whole, which is shorter than its diff:
```python
import functools

import jax
import jax.numpy as jnp
from jax import lax
from jax.experimental import pallas as pl
from jax.experimental.pallas import tpu as pltpu
from jax.sharding import PartitionSpec as P


HEAD_DIM = 128
ROPE_THETA = 1000000.0
NORM_EPS = 1e-05
NEG_LARGE = -1e30
LOG2E = 1.4426950408889634
CONTRACT_ROWS = (((0,), (0,)), ((), ()))
CONTRACT_COLS = (((1,), (1,)), ((), ()))
VMEM_LIMIT = 60 * 1024 * 1024
F32 = jnp.float32
BF16 = jnp.bfloat16


def fit(size, want):
    while size % want:
        want //= 2
    return want


def rope_tables(positions):
    inv_freq = ROPE_THETA ** (-jnp.arange(0, HEAD_DIM, 2).astype(F32) / HEAD_DIM)
    angles = positions.astype(F32)[:, None] * inv_freq[None, :]
    cos_t, sin_t = jnp.cos(angles), jnp.sin(angles)
    return jnp.concatenate([cos_t, cos_t], axis=-1), jnp.concatenate([-sin_t, sin_t], axis=-1)


def dot(a, b):
    return jnp.dot(a, b, preferred_element_type=F32)


def dot_nt(a, b):
    return lax.dot_general(a, b, CONTRACT_COLS, preferred_element_type=F32)


def rotate(values, cos_t, sin_t):
    return values * cos_t + pltpu.roll(values, HEAD_DIM // 2, 1) * sin_t


def params(n_axes):
    return pltpu.CompilerParams(dimension_semantics=("arbitrary",) * n_axes, vmem_limit_bytes=VMEM_LIMIT)


def qkv_kernel(group, h_ref, w_ref, cos_ref, sin_ref, q_ref, k_ref, kt_ref, v_ref, vt_ref):
    cos_t, sin_t = cos_ref[...], sin_ref[...]
    proj = dot(h_ref[...], w_ref[...])
    for g in range(group):
        lanes = slice(g * HEAD_DIM, (g + 1) * HEAD_DIM)
        q_ref[:, lanes] = rotate(proj[:, lanes], cos_t, sin_t).astype(BF16)
    key = rotate(proj[:, group * HEAD_DIM:(group + 1) * HEAD_DIM], cos_t, sin_t)
    k_ref[...] = key.astype(BF16)
    kt_ref[...] = key.T.astype(BF16)
    val = proj[:, (group + 1) * HEAD_DIM:]
    v_ref[...] = val.astype(BF16)
    vt_ref[...] = val.T.astype(BF16)


def project(h_all, w_all, cos_t, sin_t, group):
    seq, width = h_all.shape
    rows = fit(seq, 512)
    hd = HEAD_DIM
    return pl.pallas_call(
        functools.partial(qkv_kernel, group),
        grid=(seq // rows,),
        in_specs=[pl.BlockSpec((rows, width), lambda i: (i, 0)),
                  pl.BlockSpec((width, (group + 2) * hd), lambda i: (0, 0)),
                  pl.BlockSpec((rows, hd), lambda i: (i, 0)),
                  pl.BlockSpec((rows, hd), lambda i: (i, 0))],
        out_specs=[pl.BlockSpec((rows, group * hd), lambda i: (i, 0)),
                   pl.BlockSpec((rows, hd), lambda i: (i, 0)),
                   pl.BlockSpec((hd, rows), lambda i: (0, i)),
                   pl.BlockSpec((rows, hd), lambda i: (i, 0)),
                   pl.BlockSpec((hd, rows), lambda i: (0, i))],
        out_shape=[jax.ShapeDtypeStruct((seq, group * hd), BF16),
                   jax.ShapeDtypeStruct((seq, hd), BF16),
                   jax.ShapeDtypeStruct((hd, seq), BF16),
                   jax.ShapeDtypeStruct((seq, hd), BF16),
                   jax.ShapeDtypeStruct((hd, seq), BF16)],
        compiler_params=params(1),
        cost_estimate=pl.CostEstimate(flops=2 * seq * width * (group + 2) * hd, bytes_accessed=2 * seq * width, transcendentals=0),
        name="qkv_proj",
    )(h_all, w_all, cos_t, sin_t)


def do_kernel(group, dy_ref, w_ref, o_ref, do_ref, delta_ref):
    do = dot_nt(dy_ref[...], w_ref[...]).astype(BF16)
    do_ref[...] = do
    prod = do.astype(F32) * o_ref[...].astype(F32)
    for g in range(group):
        delta_ref[g] = jnp.sum(prod[:, g * HEAD_DIM:(g + 1) * HEAD_DIM].T, axis=0, keepdims=True)


def project_do(dy_all, wo_rows, o, group):
    seq, width = dy_all.shape
    rows = fit(seq, 512)
    gw = group * HEAD_DIM
    return pl.pallas_call(
        functools.partial(do_kernel, group),
        grid=(seq // rows,),
        in_specs=[pl.BlockSpec((rows, width), lambda i: (i, 0)),
                  pl.BlockSpec((gw, width), lambda i: (0, 0)),
                  pl.BlockSpec((rows, gw), lambda i: (i, 0))],
        out_specs=[pl.BlockSpec((rows, gw), lambda i: (i, 0)),
                   pl.BlockSpec((group, 1, rows), lambda i: (0, 0, i))],
        out_shape=[jax.ShapeDtypeStruct((seq, gw), BF16),
                   jax.ShapeDtypeStruct((group, 1, seq), F32)],
        compiler_params=params(1),
        cost_estimate=pl.CostEstimate(flops=2 * seq * width * gw, bytes_accessed=2 * seq * width, transcendentals=0),
        name="do_proj",
    )(dy_all, wo_rows, o)


def fwd_kernel(sub, bk, q_ref, k_ref, vt_ref, o_ref, lse_ref, m_ref, l_ref, acc_ref):
    i = pl.program_id(1)
    bq = q_ref.shape[0]
    n_sub = bq // sub
    c = HEAD_DIM ** -0.5 * LOG2E
    m_ref[...] = jnp.full(m_ref.shape, NEG_LARGE, F32)
    l_ref[...] = jnp.zeros(l_ref.shape, F32)
    acc_ref[...] = jnp.zeros(acc_ref.shape, F32)

    def scores(u, k):
        return dot_nt(k, q_ref[u * sub:(u + 1) * sub, :])

    def absorb(u, st, vt):
        cols = slice(u * sub, (u + 1) * sub)
        m_old = m_ref[:, cols]
        m_new = jnp.maximum(m_old, jnp.max(st, axis=0, keepdims=True) * c)
        p = jnp.exp2(st * c - m_new)
        alpha = jnp.exp2(m_old - m_new)
        m_ref[:, cols] = m_new
        l_ref[:, cols] = l_ref[:, cols] * alpha + jnp.sum(p, axis=0, keepdims=True)
        acc_ref[:, cols] = acc_ref[:, cols] * alpha + dot(vt, p.astype(BF16))

    def full_block(j, carry):
        start = pl.multiple_of(j * bk, bk)
        k = k_ref[pl.ds(start, bk), :]
        vt = vt_ref[:, pl.ds(start, bk)]
        st = scores(0, k)
        for u in range(n_sub):
            nxt = scores(u + 1, k) if u + 1 < n_sub else None
            absorb(u, st, vt)
            st = nxt
        return carry

    lax.fori_loop(0, i * (bq // bk), full_block, 0)

    base = pl.multiple_of(i * bq, bq)

    def diag_scores(u):
        rows = (u + 1) * sub
        st = scores(u, k_ref[pl.ds(base, rows), :])
        r = lax.broadcasted_iota(jnp.int32, (rows, sub), 0)
        s = lax.broadcasted_iota(jnp.int32, (rows, sub), 1) + u * sub
        return jnp.where(r <= s, st, NEG_LARGE)

    st = diag_scores(0)
    for u in range(n_sub):
        nxt = diag_scores(u + 1) if u + 1 < n_sub else None
        absorb(u, st, vt_ref[:, pl.ds(base, (u + 1) * sub)])
        st = nxt
    for u in range(n_sub):
        cols = slice(u * sub, (u + 1) * sub)
        l = l_ref[:, cols]
        o_ref[cols, :] = (acc_ref[:, cols] * (1.0 / l)).T.astype(BF16)
        lse_ref[:, cols] = m_ref[:, cols] + jnp.log2(l)


def attention_fwd(q, k, vt, group):
    seq, hd = k.shape
    bq = fit(seq, 1024)
    bk, sub = fit(bq, 512), fit(bq, 256)
    return pl.pallas_call(
        functools.partial(fwd_kernel, sub, bk),
        grid=(group, seq // bq),
        in_specs=[pl.BlockSpec((bq, hd), lambda g, i: (i, g)),
                  pl.BlockSpec((seq, hd), lambda g, i: (0, 0)),
                  pl.BlockSpec((hd, seq), lambda g, i: (0, 0))],
        out_specs=[pl.BlockSpec((bq, hd), lambda g, i: (i, g)),
                   pl.BlockSpec((None, 1, bq), lambda g, i: (g, 0, i))],
        out_shape=[jax.ShapeDtypeStruct((seq, group * hd), BF16),
                   jax.ShapeDtypeStruct((group, 1, seq), F32)],
        scratch_shapes=[pltpu.VMEM((1, bq), F32), pltpu.VMEM((1, bq), F32), pltpu.VMEM((hd, bq), F32)],
        compiler_params=params(2),
        cost_estimate=pl.CostEstimate(flops=2 * group * seq * seq * hd, bytes_accessed=8 * seq * hd * group, transcendentals=group * seq * seq // 2),
        name="attn_fwd",
    )(q, k, vt)


def bwd_kernel(n_prev, half, q_ref, do_ref, k_ref, kt_ref, v_ref, lse_ref, delta_ref, cos_ref, sin_ref, *refs):
    if n_prev:
        dkp_ref, dvp_ref, out_ref, dqt_ref, dk_ref, dv_ref = refs
    else:
        dq_ref, dk_out, dv_out, dqt_ref, dk_ref, dv_ref = refs
    j = pl.program_id(1)
    n = pl.num_programs(1)
    bk = k_ref.shape[0]
    c = HEAD_DIM ** -0.5 * LOG2E

    @pl.when(j == 0)
    def _():
        dqt_ref[...] = jnp.zeros(dqt_ref.shape, F32)

    if n_prev:
        dk_ref[...] = sum(dkp_ref[p] for p in range(n_prev))
        dv_ref[...] = sum(dvp_ref[p] for p in range(n_prev))
    else:
        dk_ref[...] = jnp.zeros(dk_ref.shape, F32)
        dv_ref[...] = jnp.zeros(dv_ref.shape, F32)

    def block(start, width, lo, masked):
        cols = pl.ds(start, width)
        qb, dob = q_ref[cols, :], do_ref[cols, :]
        st = dot_nt(k_ref[lo:, :], qb)
        dpt = dot_nt(v_ref[lo:, :], dob)
        p = jnp.exp2(st * c - lse_ref[:, cols])
        if masked:
            r = lax.broadcasted_iota(jnp.int32, p.shape, 0)
            s = lax.broadcasted_iota(jnp.int32, p.shape, 1)
            p = jnp.where(r <= s, p, 0.0)
        ds = (p * (dpt - delta_ref[:, cols])).astype(BF16)
        pb = p.astype(BF16)
        dv_ref[lo:, :] += dot(pb, dob)
        dk_ref[lo:, :] += dot(ds, qb)
        dqt_ref[:, cols] += dot(kt_ref[:, lo:], ds)

    own = pl.multiple_of(j * bk, bk)
    if half:
        rest = bk - half

        def first_half():
            cols = pl.ds(own, bk)
            qb, dob = q_ref[cols, :], do_ref[cols, :]
            st = dot_nt(k_ref[:half, :], qb)
            dpt = dot_nt(v_ref[:half, :], dob)
            r = lax.broadcasted_iota(jnp.int32, st.shape, 0)
            s = lax.broadcasted_iota(jnp.int32, st.shape, 1)
            p = jnp.where(r <= s, jnp.exp2(st * c - lse_ref[:, cols]), 0.0)
            ds = (p * (dpt - delta_ref[:, cols])).astype(BF16)
            pb = p.astype(BF16)
            dv_ref[:half, :] += dot(pb, dob)
            dk_ref[:half, :] += dot(ds, qb)
            dqt_ref[:, cols] += dot(kt_ref[:, :half], ds)

        first_half()
        block(pl.multiple_of(own + half, half), rest, half, True)
    else:
        block(own, bk, 0, True)

    left = n - 1 - j
    pairs = left // 2

    def pair_body(t, carry):
        start = pl.multiple_of((j + 1 + 2 * t) * bk, bk)
        block(start, 2 * bk, 0, False)
        return carry

    lax.fori_loop(0, pairs, pair_body, 0)

    @pl.when(left % 2 == 1)
    def _():
        block(pl.multiple_of((n - 1) * bk, bk), bk, 0, False)

    scale = HEAD_DIM ** -0.5
    cos_t, sin_t = cos_ref[...], -sin_ref[...]
    dq = rotate(dqt_ref[:, pl.ds(own, bk)].T * scale, cos_t, sin_t).astype(BF16)
    if n_prev:
        hd = HEAD_DIM
        out_ref[:, :hd] = dq
        out_ref[:, hd:2 * hd] = rotate(dk_ref[...] * scale, cos_t, sin_t).astype(BF16)
        out_ref[:, 2 * hd:] = dv_ref[...].astype(BF16)
    else:
        dq_ref[...] = dq
        dk_out[...] = dk_ref[...]
        dv_out[...] = dv_ref[...]


def attention_bwd(first, heads, q, do, k, kt, v, lse, delta, cos_t, sin_t, prev=None):
    seq, hd = k.shape
    bk = fit(seq, 512)
    half = bk // 2 if bk % 256 == 0 else 0
    n_prev = 0 if prev is None else prev[0].shape[0]
    whole = pl.BlockSpec((seq, hd), lambda g, j: (0, first + g))
    row = pl.BlockSpec((None, 1, seq), lambda g, j: (first + g, 0, 0))
    blk = pl.BlockSpec((bk, hd), lambda g, j: (j, 0))
    in_specs = [whole, whole, blk, pl.BlockSpec((hd, bk), lambda g, j: (0, j)), blk, row, row, blk, blk]
    args = [q, do, k, kt, v, lse, delta, cos_t, sin_t]
    if prev is None:
        part = pl.BlockSpec((None, bk, hd), lambda g, j: (g, j, 0))
        out_specs = [pl.BlockSpec((bk, hd), lambda g, j: (j, g)), part, part]
        out_shape = [jax.ShapeDtypeStruct((seq, heads * hd), BF16)] + [jax.ShapeDtypeStruct((heads, seq, hd), F32)] * 2
    else:
        part = pl.BlockSpec((n_prev, bk, hd), lambda g, j: (0, j, 0))
        in_specs += [part, part]
        args += list(prev)
        out_specs = pl.BlockSpec((bk, 3 * hd), lambda g, j: (j, 0))
        out_shape = jax.ShapeDtypeStruct((seq, 3 * hd), BF16)
    return pl.pallas_call(
        functools.partial(bwd_kernel, n_prev, half),
        grid=(heads, seq // bk),
        in_specs=in_specs,
        out_specs=out_specs,
        out_shape=out_shape,
        scratch_shapes=[pltpu.VMEM((hd, seq), F32), pltpu.VMEM((bk, hd), F32), pltpu.VMEM((bk, hd), F32)],
        compiler_params=params(2),
        cost_estimate=pl.CostEstimate(flops=5 * heads * seq * seq * hd, bytes_accessed=16 * seq * hd * heads, transcendentals=heads * seq * seq // 2),
        name="attn_bwd_last" if n_prev else "attn_bwd",
    )(*args)


def assemble_q_kernel(a_ref, b_ref, wq_ref):
    first = a_ref.shape[1]
    wq_ref[:, :first] = a_ref[...]
    wq_ref[:, first:] = b_ref[...]


def assemble_q(early, late):
    parts, rows, first = early.shape
    second = late.shape[2]
    br = fit(rows, 1024)
    return pl.pallas_call(
        assemble_q_kernel,
        grid=(parts, rows // br),
        in_specs=[pl.BlockSpec((None, br, first), lambda s, r: (s, r, 0)),
                  pl.BlockSpec((None, br, second), lambda s, r: (s, r, 0))],
        out_specs=pl.BlockSpec((br, first + second), lambda s, r: (r, s)),
        out_shape=jax.ShapeDtypeStruct((rows, parts * (first + second)), F32),
        compiler_params=params(2),
        cost_estimate=pl.CostEstimate(flops=parts * rows * 1024, bytes_accessed=8 * parts * rows * (first + second), transcendentals=0),
        name="assemble_dwq",
    )(early, late)


def assemble_kv_kernel(a_ref, wk_ref, wv_ref):
    hd = HEAD_DIM
    wk_ref[...] = a_ref[:, :hd]
    wv_ref[...] = a_ref[:, hd:]


def assemble_kv(both):
    parts, rows, _ = both.shape
    hd = HEAD_DIM
    br = fit(rows, 1024)
    out = pl.BlockSpec((br, hd), lambda s, r: (r, s))
    return pl.pallas_call(
        assemble_kv_kernel,
        grid=(parts, rows // br),
        in_specs=[pl.BlockSpec((None, br, 2 * hd), lambda s, r: (s, r, 0))],
        out_specs=[out, out],
        out_shape=[jax.ShapeDtypeStruct((rows, parts * hd), F32)] * 2,
        compiler_params=params(2),
        cost_estimate=pl.CostEstimate(flops=parts * rows * 1024, bytes_accessed=8 * parts * rows * 2 * hd, transcendentals=0),
        name="assemble_dwkv",
    )(both)


def copy_kernel(a_ref, b_ref):
    b_ref[...] = a_ref[...]


def copy_out(a):
    rows, cols = a.shape
    br = fit(rows, 256)
    spec = pl.BlockSpec((br, cols), lambda i: (i, 0))
    return pl.pallas_call(
        copy_kernel, grid=(rows // br,), in_specs=[spec], out_specs=spec,
        out_shape=jax.ShapeDtypeStruct(a.shape, a.dtype), compiler_params=params(1),
        cost_estimate=pl.CostEstimate(flops=rows * 1024, bytes_accessed=8 * rows * cols, transcendentals=0),
        name="copy_dwo",
    )(a)


def solution(mesh):
    sp_size = mesh.shape['sp']
    seq_spec = P(('dp', 'sp'), None)
    pos_spec = P(('dp', 'sp'))
    replicated = P(None, None)
    part_rows = P('dp', None)

    def local_step(x, grad_out, positions, gain, w_q, w_k, w_v, w_o):
        tok, width = x.shape
        hd = HEAD_DIM
        group = w_q.shape[1] // hd // sp_size
        assert w_k.shape[1] // hd == sp_size and group >= 2
        gw = group * hd
        me = lax.axis_index('sp')

        x_f = x.astype(F32)
        inv_rms = lax.rsqrt(jnp.mean(x_f * x_f, axis=-1, keepdims=True) + NORM_EPS)
        normed = x_f * inv_rms
        gain_f = gain.astype(F32)
        hidden = (normed * gain_f).astype(BF16)
        h_all = lax.all_gather(hidden, 'sp', axis=0, tiled=True)

        pos_all = lax.all_gather(positions, 'sp', axis=0, tiled=True)
        cos_t, sin_t = rope_tables(pos_all)
        w_all = jnp.concatenate([lax.dynamic_slice(w_q, (0, me * gw), (width, gw)),
                                 lax.dynamic_slice(w_k, (0, me * hd), (width, hd)),
                                 lax.dynamic_slice(w_v, (0, me * hd), (width, hd))], axis=1)
        wo_rows = lax.dynamic_slice(w_o, (me * gw, 0), (gw, width))

        dy_late, _, cos_t, sin_t, w_all, wo_rows = lax.optimization_barrier((grad_out, hidden, cos_t, sin_t, w_all, wo_rows))
        dy_all = lax.all_gather(dy_late, 'sp', axis=0, tiled=True)

        q, k, kt, v, vt = project(h_all, w_all, cos_t, sin_t, group)
        o, lse = attention_fwd(q, k, vt, group)

        o_loc = lax.all_to_all(o.reshape(sp_size, tok, gw), 'sp', 0, 0, tiled=True)
        wo_block = lax.dot_general(o, dy_all, CONTRACT_ROWS, preferred_element_type=F32)
        grad_wo = lax.all_gather(wo_block, 'sp', axis=0, tiled=True)
        grad_wo = copy_out(grad_wo)
        do, delta = project_do(dy_all, wo_rows, o, group)

        early = group - 1
        dq_a, dk_p, dv_p = attention_bwd(0, early, q, do, k, kt, v, lse, delta, cos_t, sin_t)
        dq_a_loc = lax.all_to_all(dq_a.reshape(sp_size, tok, early * hd), 'sp', 0, 0, tiled=True)
        dw_a = lax.dot_general(h_all, dq_a, CONTRACT_ROWS, preferred_element_type=F32)
        dw_a_all = lax.all_gather(dw_a, 'sp', axis=0)
        d_b = attention_bwd(early, 1, q, do, k, kt, v, lse, delta, cos_t, sin_t, prev=(dk_p, dv_p))
        d_b_loc = lax.all_to_all(d_b.reshape(sp_size, tok, 3 * hd), 'sp', 0, 0, tiled=True)
        dw_b = lax.dot_general(h_all, d_b[:, :hd], CONTRACT_ROWS, preferred_element_type=F32)
        dw_b_all = lax.all_gather(dw_b, 'sp', axis=0)
        dw_c = lax.dot_general(h_all, d_b[:, hd:], CONTRACT_ROWS, preferred_element_type=F32)
        dw_c_all = lax.all_gather(dw_c, 'sp', axis=0)

        o_rows = jnp.transpose(o_loc, (1, 0, 2)).reshape(tok, sp_size * gw)
        result = (x_f + dot(o_rows, w_o)).astype(BF16)

        dq_pre = jnp.transpose(jnp.concatenate([dq_a_loc, d_b_loc[:, :, :hd]], axis=-1), (1, 0, 2)).reshape(tok, sp_size * gw)
        dk_pre = jnp.transpose(d_b_loc[:, :, hd:2 * hd], (1, 0, 2)).reshape(tok, sp_size * hd)
        dv_pre = jnp.transpose(d_b_loc[:, :, 2 * hd:], (1, 0, 2)).reshape(tok, sp_size * hd)
        d_hidden = dot_nt(dq_pre, w_q) + dot_nt(dk_pre, w_k) + dot_nt(dv_pre, w_v)
        grad_gain = lax.psum(jnp.sum(d_hidden * normed, axis=0), 'sp')
        d_normed = d_hidden * gain_f
        d_xnorm = inv_rms * (d_normed - normed * jnp.mean(d_normed * normed, axis=-1, keepdims=True))
        grad_x = (grad_out.astype(F32) + d_xnorm).astype(BF16)

        grad_wq = assemble_q(dw_a_all, dw_b_all)
        grad_wk, grad_wv = assemble_kv(dw_c_all)
        return result, grad_x, grad_wq, grad_wk, grad_wv, grad_wo, grad_gain

    return jax.shard_map(local_step, mesh=mesh,
                         in_specs=(seq_spec, seq_spec, pos_spec, P(None), replicated, replicated, replicated, replicated),
                         out_specs=(seq_spec, seq_spec, part_rows, part_rows, part_rows, part_rows, P('dp')),
                         check_vma=False)
```

time: 5940 us -> 1610 us (0.27)
  matrix products: 2780 us -> 190 us
  other arithmetic: 1610 us -> 59.1 us
  Pallas kernels: 0 us -> 744 us
  waiting for transfers between devices: 1150 us -> 478 us
  local copies, waits for them, and re-layouts: 286 us -> 39.4 us
    dot_general x124 -> x8, matrix products: 2780 us -> 190 us  [the longest x3 59.8 us: dot_nt(): return lax.dot_general(a, b, CONTRACT_COLS, preferred_element_type=F32)]
    psum x1 -> x0, waiting for transfers between devices: 987 us -> none  [local_step(): lax.psum(lax.dot_general(hidden, dq_pre, CONTRACT_ROWS, preferred_element...]
    reduce_sum x33 -> x0, other arithmetic: 745 us -> none  [the longest x32 736 us: one_block(): attn_prob = jax.nn.softmax(jnp.where(causal, scores, NEG_LARGE), axis=-1)]
    pallas_call x0 -> x8, Pallas kernels: none -> 744 us  [the longest x2 321 us: attention_bwd(): pl.pallas_call(functools.partial(bwd_kernel, n_prev, half), grid=(heads,...]
    another operation x20 -> x0, other arithmetic: 687 us -> none
    all_gather x0 -> x6, waiting for transfers between devices: none -> 347 us  [the longest x1 179 us: local_step(): h_all = lax.all_gather(hidden, 'sp', axis=0, tiled=True)]
    unnamed x65 -> x22, local copies, waits for them, and re-layouts: 129 us -> 1.82 us
    ge x32 -> x0, other arithmetic: 102 us -> none  [one_block(): causal = (blk_start + jnp.arange(row_count))[:, None] >= key_index[None, :]]
  transfers between devices with their start and end apart: 9 -> 9, of which waited for: 6 -> 5; matrix products, arithmetic and copies ran while one was open for 26% -> 16% of each run, Pallas kernels for 0% -> 23%
where the time goes in v1:
time: 1610 us; the launch traced here: 1600 us
  Pallas kernels  744 us (46%)
  waiting for transfers between devices  478 us (30%)
  matrix products  190 us (12%)
  other arithmetic  59.1 us (4%)
  blocking collectives  54.6 us (3%)
  local copies, waits for them, and re-layouts  39.4 us (2%)
  starting transfers between devices  17.8 us (1%)
    pallas_call x2, Pallas kernels, attention_bwd(): pl.pallas_call(functools.partial(bwd_kernel, n_prev, half), grid=(heads,...  321 us
    pallas_call x1, Pallas kernels, attention_fwd(): pl.pallas_call(functools.partial(fwd_kernel, sub, bk), grid=(group, seq /...  250 us
    all_gather x1, waiting for transfers between devices, local_step(): h_all = lax.all_gather(hidden, 'sp', axis=0, tiled=True)  179 us
    all_gather x1, waiting for transfers between devices, local_step(): grad_wo = lax.all_gather(wo_block, 'sp', axis=0, tiled=True)  142 us
    all_to_all x1, waiting for transfers between devices, local_step(): lax.all_to_all(d_b.reshape(sp_size, tok, 3 * hd), 'sp', 0, 0, tiled=True)  83.2 us
    dot_general x3, matrix products, dot_nt(): return lax.dot_general(a, b, CONTRACT_COLS, preferred_element_type=F32)  59.8 us
    pallas_call x1, Pallas kernels, project(): pl.pallas_call(functools.partial(qkv_kernel, group), grid=(seq // rows,),...  50.1 us
    all_to_all x1, waiting for transfers between devices, local_step(): lax.all_to_all(dq_a.reshape(sp_size, tok, early * hd), 'sp', 0, 0, tiled=...  47.7 us
  transfers between devices with their start and end apart: 9, of which 5 were waited for; matrix products, arithmetic and copies ran while one was open for 16% of the time, Pallas kernels for 23%

profile of v1, /device:TPU:1, one launch (start us, length us, event | category | flops | bytes accessed | tf_op | source)
XLA Modules:
  0.0 1598.4 jit_solution(16197637081427735680)
XLA Ops:
  40.0 18.0 %fusion.17 = (f32[8192,64]{1,0:T(8,128)S(1)}, f32[8192,64]{1,0:T(8,128)}, f32[8192,64]{1,0:T(8,128)}) fusion(f32[64]{0:T(128)S(1)} %multiply_power_fusion, f32[8192]{0:T(1024)S(1)} %convert_element_type.31), kind=kLoop, calls=%fused_computation.27 | loop fusion | flops 1048576 | bytes 6324480 | tf_op jit(solution)/shard_map/neg | solution.py:33
  68.2 178.8 %all-gather.10.cloned.1.call-done.h_ref = bf16[8192,3072]{1,0:T(8,128)(2,1)} async-done(((bf16[1024,3072]{1,0:T(8,128)(2,1)}), bf16[8192,3072]{1,0:T(8,128)(2,1)}) %all-gather.10.cloned.1.call-update) | async-done | bytes 50331664 | tf_op jit(solution)/shard_map/all_gather | solution.py:401
  247.0 50.1 %qkv_proj.1 = (bf16[8192,384]{1,0:T(8,128)(2,1)}, bf16[8192,128]{1,0:T(8,128)(2,1)}, bf16[128,8192]{1,0:T(8,128)(2,1)}, bf16[8192,128]{1,0:T(8,128)(2,1)}, bf16[128,8192]{1,0:T(8,128)(2,1)}) custom-call(bf16[8192,3072]{1,0:T(8,128)(2,1)} %all-gather.10.cloned.1.call-done.h_ref, bf16[3072,640]{1,0:T(8,128)(2,1)} %pad_maximum_fusion.3.w_ref, ...), custom_call_target="tpu_custom_call" | custom-call | flops 32212254720 | bytes 50331648 | tf_op jit(solution)/shard_map/qkv_proj/pallas_call | solution.py:70
  297.2 250.3 %attn_fwd.1 = (bf16[8192,384]{1,0:T(8,128)(2,1)}, f32[3,1,8192]{2,1,0:T(1,128)}) custom-call(bf16[8192,384]{1,0:T(8,128)(2,1)} %get-tuple-element.29.q_ref, bf16[8192,128]{1,0:T(8,128)(2,1)} %get-tuple-element.30.k_ref, bf16[128,8192]{1,0:T(8,128)(2,1)} %get-tuple-element.31.vt_ref), custom_call_target="tpu_custom_call" | custom-call | flops 51539607552 | bytes 25165824 | tf_op jit(solution)/shard_map/attn_fwd/pallas_call | solution.py:181
  547.5 35.9 %do_proj.1 = (bf16[8192,384]{1,0:T(8,128)(2,1)}, f32[3,1,8192]{2,1,0:T(1,128)}) custom-call(bf16[8192,3072]{1,0:T(8,128)(2,1)} %all-gather.12.cloned.1.call-done.dy_ref, bf16[384,3072]{1,0:T(8,128)(2,1)} %constant_dynamic-slice_fusion.w_ref, bf16[8192,384]{1,0:T(8,128)(2,1)} %get-tuple-element.32.o_ref), custom_call_target="tpu_custom_call" | custom-call | flops 19327352832 | bytes 50331648 | tf_op jit(solution)/shard_map/do_proj/pallas_call | solution.py:105
  583.4 212.6 %attn_bwd.1 = (bf16[8192,256]{1,0:T(8,128)(2,1)}, f32[2,8192,128]{2,1,0:T(8,128)}, f32[2,8192,128]{2,1,0:T(8,128)}) custom-call(bf16[8192,384]{1,0:T(8,128)(2,1)} %get-tuple-element.29.q_ref, bf16[8192,384]{1,0:T(8,128)(2,1)} %get-tuple-element.35.do_ref, bf16[8192,128]{1,0:T(8,128)(2,1)} %get-tuple-element.30.k_ref, ...), custom_call_target="tpu_custom_call" | custom-call | flops 85899345920 | bytes 33554432 | tf_op jit(solution)/shard_map/attn_bwd/pallas_call | solution.py:306
  796.1 108.7 %attn_bwd_last.1 = bf16[8192,384]{1,0:T(8,128)(2,1)} custom-call(bf16[8192,384]{1,0:T(8,128)(2,1)} %get-tuple-element.29.q_ref, bf16[8192,384]{1,0:T(8,128)(2,1)} %get-tuple-element.35.do_ref, bf16[8192,128]{1,0:T(8,128)(2,1)} %get-tuple-element.30.k_ref, bf16[128,8192]{1,0:T(8,128)(2,1)} %get-tuple-element.36.kt_ref, ...), custom_call_target="tpu_custom_call" | custom-call | flops 42949672960 | bytes 16777216 | tf_op jit(solution)/shard_map/attn_bwd_last/pallas_call | solution.py:306
  904.8 23.8 %fusion.13 = f32[3072,256]{1,0:T(8,128)} fusion(bf16[8192,3072]{1,0:T(8,128)(2,1)} %all-gather.10.cloned.1.call-done.h_ref, bf16[8192,384]{1,0:T(8,128)(2,1)} %attn_bwd_last.1), kind=kOutput, calls=%fused_computation.20 | convolution fusion | flops 12884901888 | bytes 57671680 | tf_op jit(solution)/shard_map/dot_general | solution.py:431
  928.7 26.9 %fusion.15 = f32[3072,128]{1,0:T(8,128)} fusion(bf16[8192,3072]{1,0:T(8,128)(2,1)} %all-gather.10.cloned.1.call-done.h_ref, bf16[8192,384]{1,0:T(8,128)(2,1)} %attn_bwd_last.1), kind=kOutput, calls=%fused_computation.25 | convolution fusion | flops 6442450944 | bytes 54001664 | tf_op jit(solution)/shard_map/dot_general | solution.py:429
  955.7 23.9 %fusion.21 = f32[3072,256]{1,0:T(8,128)} fusion(bf16[8192,3072]{1,0:T(8,128)(2,1)} %all-gather.10.cloned.1.call-done.h_ref, bf16[8192,256]{1,0:T(8,128)(2,1)} %get-tuple-element.40), kind=kOutput, calls=%fused_computation.38 | convolution fusion | flops 12884901888 | bytes 57671680 | tf_op jit(solution)/shard_map/dot_general | solution.py:425
  979.7 28.9 %fusion.22 = f32[384,3072]{1,0:T(8,128)} fusion(bf16[8192,384]{1,0:T(8,128)(2,1)} %get-tuple-element.32.o_ref, bf16[8192,3072]{1,0:T(8,128)(2,1)} %all-gather.12.cloned.1.call-done.dy_ref), kind=kOutput, calls=%fused_computation.39 | convolution fusion | flops 19327352832 | bytes 61341696 | tf_op jit(solution)/shard_map/dot_general | solution.py:417
  1027.5 83.2 %all-to-all-done.2 = bf16[8,1024,384]{1,2,0:T(8,128)(2,1)} async-done(((bf16[8,1024,384]{1,2,0:T(8,128)(2,1)}), bf16[8,1024,384]{1,2,0:T(8,128)(2,1)}, u32[]{:S(2)}, u32[]{:S(2)}) %all-to-all-start.2) | async-done | bytes 6291488 | tf_op jit(solution)/shard_map/all_to_all | solution.py:428
  1131.8 47.7 %all-to-all-done.1 = bf16[8,1024,256]{1,2,0:T(8,128)(2,1)} async-done(((bf16[8,1024,256]{1,2,0:T(8,128)(2,1)}), bf16[8,1024,256]{1,2,0:T(8,128)(2,1)}, u32[]{:S(2)}, u32[]{:S(2)}) %all-to-all-start.1) | async-done | bytes 4194336 | tf_op jit(solution)/shard_map/all_to_all | solution.py:424
  1192.6 12.7 fusion.20
  1205.3 12.7 fusion.19
  1218.0 34.5 %fusion.10 = (f32[3072]{0:T(1024)S(1)}, f32[1024]{0:T(1024)S(1)}, f32[1024,3072]{1,0:T(8,128)}) fusion(bf16[1024,3072]{1,0:T(8,128)(2,1)S(1)} %bitcast.33, f32[1024]{0:T(1024)S(1)} %copy-done.6, f32[3072]{0:T(1024)S(1)} %copy-done.4, f32[1024,3072]{1,0:T(8,128)} %fusion.20, f32[1024,3072]{1,0:T(8,128)} %fusion.19, bf16[1024,3072]{0,1:T(8,128)(2,1)} %bitcast.39, ...), kind=kOutput, calls=%fused_computation.13 | convolution fusion | flops 19355660288 | bytes 69238784 | tf_op jit(solution)/shard_map/dot_general | solution.py:41
  1252.5 43.6 %psum.7 = f32[3072]{0:T(1024)} all-reduce(f32[3072]{0:T(1024)S(1)} %get-tuple-element.45), channel_id=1, replica_groups=mesh['dp'=1,'sp'=8] {'sp'}, use_global_device_ids=true, to_apply=%region_3.0 | all-reduce | flops 3072 | bytes 24576 | tf_op jit(solution)/shard_map/psum | solution.py:441
  1296.1 13.1 fusion.9
  1309.3 26.7 %fusion.12 = bf16[1024,3072]{1,0:T(8,128)(2,1)} fusion(bf16[1024,3072]{1,0:T(8,128)(2,1)} %param.8, bf16[1024,3072]{0,1:T(8,128)(2,1)} %bitcast.2, bf16[3072,3072]{1,0:T(8,128)(2,1)} %param.15), kind=kOutput, calls=%fused_computation.15 | convolution fusion | flops 19336790016 | bytes 37748736 | tf_op jit(solution)/shard_map/dot_general | solution.py:37
  1335.9 25.9 %assemble_dwkv.1 = (f32[3072,1024]{1,0:T(8,128)}, f32[3072,1024]{1,0:T(8,128)}) custom-call(f32[8,3072,256]{2,1,0:T(8,128)} %bitcast.34), custom_call_target="tpu_custom_call" | custom-call | flops 25165824 | bytes 50331648 | tf_op jit(solution)/shard_map/assemble_dwkv/pallas_call | solution.py:353
  1361.9 26.3 %all-gather.16.cloned.1.call-done = f32[24576,256]{1,0:T(8,128)} async-done(((f32[3072,256]{1,0:T(8,128)}), f32[24576,256]{1,0:T(8,128)}) %all-gather.16.cloned.1.call-update) | async-done | bytes 25165840 | tf_op jit(solution)/shard_map/all_gather | solution.py:426
  1388.2 33.5 %assemble_dwq.1 = f32[3072,3072]{1,0:T(8,128)} custom-call(f32[8,3072,256]{2,1,0:T(8,128)} %bitcast.35, f32[8,3072,128]{2,1,0:T(8,128)} %bitcast.36), custom_call_target="tpu_custom_call" | custom-call | flops 25165824 | bytes 75497472 | tf_op jit(solution)/shard_map/assemble_dwq/pallas_call | solution.py:329
  1421.6 142.2 %all-gather.14.cloned.1.call-done.a_ref = f32[3072,3072]{1,0:T(8,128)} async-done(((f32[384,3072]{1,0:T(8,128)}), f32[3072,3072]{1,0:T(8,128)}) %all-gather.14.cloned.1.call-update) | async-done | bytes 37748752 | tf_op jit(solution)/shard_map/all_gather | solution.py:418
  1563.8 27.3 %copy_dwo.1 = f32[3072,3072]{1,0:T(8,128)} custom-call(f32[3072,3072]{1,0:T(8,128)} %all-gather.14.cloned.1.call-done.a_ref), custom_call_target="tpu_custom_call" | custom-call | flops 3145728 | bytes 75497472 | tf_op jit(solution)/shard_map/copy_dwo/pallas_call | solution.py:373
  (60 shorter events, 96.3 us)
Async XLA Ops:
  7.2 4.3 copy-start.7
  7.2 239.9 %all-gather.10.cloned.1.call-start = ((), (), s32[]{:S(2)}) async-start(), calls=%async_computation.3 | async-start | bytes 56623104 | tf_op jit(solution)/shard_map/all_gather | solution.py:401
  7.2 5.5 copy-start
  11.5 0.6 copy-start.5
  12.1 0.6 copy-start.3
  18.1 0.7 copy-start.8
  18.1 529.4 %all-gather.12.cloned.1.call-start = ((), (), s32[]{:S(2)}) async-start(), calls=%async_computation.4 | async-start | bytes 56623104 | tf_op jit(solution)/shard_map/all_gather | solution.py:411
  68.2 1267.8 %all-gather.20.cloned.1.call-start = ((), (), s32[]{:S(2)}) async-start(), calls=%async_computation.8 | async-start | bytes 28311552 | tf_op jit(solution)/shard_map/all_gather | solution.py:432
  928.7 433.2 %all-gather.18.cloned.1.call-start = ((), (), s32[]{:S(2)}) async-start(), calls=%async_computation.7 | async-start | bytes 14155776 | tf_op jit(solution)/shard_map/all_gather | solution.py:430
  955.7 432.5 %all-gather.16.cloned.1.call-start = ((), (), s32[]{:S(2)}) async-start(), calls=%async_computation.6 | async-start | bytes 28311552 | tf_op jit(solution)/shard_map/all_gather | solution.py:426
  979.7 584.1 %all-gather.14.cloned.1.call-start = ((), (), s32[]{:S(2)}) async-start(), calls=%async_computation.5 | async-start | bytes 42467328 | tf_op jit(solution)/shard_map/all_gather | solution.py:418
  1017.3 93.4 %all-to-all-start.2 = ((bf16[8,1024,384]{1,2,0:T(8,128)(2,1)}), bf16[8,1024,384]{1,2,0:T(8,128)(2,1)}, u32[]{:S(2)}, u32[]{:S(2)}) async-start(bf16[8,1024,384]{1,2,0:T(8,128)(2,1)} %copy.20), calls=%async_computation.2 | async-start | bytes 12582912 | tf_op jit(solution)/shard_map/all_to_all | solution.py:428
  1110.7 68.8 %all-to-all-start.1 = ((bf16[8,1024,256]{1,2,0:T(8,128)(2,1)}), bf16[8,1024,256]{1,2,0:T(8,128)(2,1)}, u32[]{:S(2)}, u32[]{:S(2)}) async-start(bf16[8,1024,256]{1,2,0:T(8,128)(2,1)} %copy.19), calls=%async_computation.1 | async-start | bytes 8388608 | tf_op jit(solution)/shard_map/all_to_all | solution.py:424
  1179.4 129.8 %all-to-all-start = ((bf16[8,1024,384]{1,2,0:T(8,128)(2,1)}), bf16[8,1024,384]{1,2,0:T(8,128)(2,1)}, u32[]{:S(2)}, u32[]{:S(2)}) async-start(bf16[8,1024,384]{1,2,0:T(8,128)(2,1)} %copy.18), calls=%async_computation | async-start | bytes 12582912 | tf_op jit(solution)/shard_map/all_to_all | solution.py:416
  1186.7 6.0 copy-start.2
  1192.6 12.7 copy-start.1
  1192.6 25.4 %slice-start = ((s8[6291456]{0:T(1024)(128)(4,1)}), s8[4194304]{0:T(1024)(128)(4,1)S(1)}, s32[]{:S(2)}) async-start(s8[6291456]{0:T(1024)(128)(4,1)} %bitcast.32), calls=%async_computation.9 | async-start | bytes 8388608
  1205.3 12.7 slice-start.1
  1205.3 12.7 copy-start.4
  1205.3 12.7 copy-start.6
Sparse Core Ops, SparseCore 0:
  18.3 228.7 all-gather.9
  248.9 226.5 all-gather.11
  928.8 157.9 all-gather.19
  1088.4 161.1 all-gather.17
  1251.3 136.8 all-gather.15
  1389.9 173.8 all-gather.13
